TPU v7x, 256 devices: a whole 4x4x8 slice. The times are simulated.
256 devices in a mesh: dp: 64 (over x, z, core), mp: 4 (over y).
Axes of the slice: x: 4, y: 4, z: 8, core: 2. Of those that a mesh axis runs over, the one named last changes fastest.
Arguments:
- sparse_vecs: bfloat16 [65536, 26, 128], P(('dp', 'mp')), may hold values from -6 to 6
- dense_vec: bfloat16 [65536, 128], P(('dp', 'mp')), may hold values from -6 to 6
- top_cot: bfloat16 [65536, 1024], P(('dp', 'mp')), may hold values from -0.59765625 to 0.59765625
- top_weight: bfloat16 [479, 1024], replicated, may hold values from -0.25 to 0.25
- owner_ids: int32 [65536, 26, 1], P(('dp', 'mp')), may hold values from 0 to 63; in each aligned block of 6656 rows (0 to 6655, 6656 to 13311, ..., all dimensions but the last counted through in order) at most 208 rows name the same one
- local_rows: int32 [65536, 26], P(('dp', 'mp')), may hold values from 0 to 127
- table: float32 [26, 8192, 128], P(None, ('dp', 'mp')), may hold values from -0.6 to 0.6
- accum: float32 [26, 8192], P(None, ('dp', 'mp')), may hold values from 0.05 to 2
Outputs:
- dense_grad: bfloat16 [65536, 128], P(('dp', 'mp'))
- new_table: float32 [26, 8192, 128], P(None, ('dp', 'mp'))
- new_accum: float32 [26, 8192], P(None, ('dp', 'mp'))
Inputs may be any that keep to these rules, and one draw needn't show every extreme that they name: `owner_ids`: among the lookups of one device's 256 samples no owner group is named more than 208 times; in every draw some device names some owner group exactly 208 times.
All inputs are finite; a program needn't handle non-finite values.
Results may differ from a plain program's by a relative error of at most 0.005.
Values may be sent and summed in bfloat16 or wider, within the bound.
A program may use at most 128 MiB of HBM per device.

v0:
```python
import jax
import jax.numpy as jnp
import numpy as np
from jax import lax
from jax.sharding import PartitionSpec as P

LEARN_RATE = 0.1
EPSILON = 1e-08


def split_up(x, dim, length):
    before, after = (x.shape[:dim], x.shape[dim + 1 :])
    return jnp.moveaxis(x.reshape(*before, length, -1, *after), dim, 0)


def sent_and_summed(x, axis, dim):
    pieces = split_up(x, dim, lax.axis_size(axis))
    arrived = lax.all_to_all(pieces, axis, split_axis=0, concat_axis=0, tiled=True)
    return arrived.astype(jnp.float32).sum(axis=0)


def pair_matrix(feature_count):
    row_index, col_index = np.tril_indices(feature_count, -1)
    pair_count = row_index.shape[0]
    matrix = np.zeros((pair_count, feature_count * feature_count), np.float32)
    matrix[np.arange(pair_count), row_index * feature_count + col_index] = 1.0
    matrix[np.arange(pair_count), col_index * feature_count + row_index] = 1.0
    return jnp.asarray(matrix)


def accumulate(grad_rows, grad_keys, first_col, columns):
    sources, capacity, row_width = grad_rows.shape
    most_rows = max(1, 4096 // capacity)
    per_turn = 1
    while per_turn * 2 <= most_rows and sources % (per_turn * 2) == 0:
        per_turn = per_turn * 2
    turn_count = sources // per_turn
    row_blocks = grad_rows.reshape(turn_count, per_turn * capacity, row_width)
    key_blocks = grad_keys.reshape(turn_count, per_turn * capacity) - first_col
    targets = jnp.arange(columns, dtype=jnp.int32)[None, :]

    def add_block(turn_index, running):
        row_piece = lax.dynamic_index_in_dim(row_blocks, turn_index, 0, keepdims=False)
        key_piece = lax.dynamic_index_in_dim(key_blocks, turn_index, 0, keepdims=False)
        onehot = (key_piece[:, None] == targets).astype(jnp.bfloat16)
        return running + lax.dot_general(
            onehot, row_piece, (((0,), (0,)), ((), ())), preferred_element_type=jnp.float32
        )

    return lax.fori_loop(0, turn_count, add_block, jnp.zeros((columns, row_width), jnp.float32))


def slot_ranks(target, dp_count):
    lookups = target.shape[0]
    block_len = min(512, lookups)
    block_count = (lookups + block_len - 1) // block_len
    padded_len = block_count * block_len
    padded_target = jnp.concatenate([target, jnp.full((padded_len - lookups,), -1, jnp.int32)])
    member = (padded_target[:, None] == jnp.arange(dp_count, dtype=jnp.int32)[None, :]).astype(
        jnp.bfloat16
    )
    member_blocks = member.reshape(block_count, block_len, dp_count)
    lower = (jnp.arange(block_len)[:, None] >= jnp.arange(block_len)[None, :]).astype(jnp.bfloat16)
    within = jnp.einsum("ij,bjd->bid", lower, member_blocks, preferred_element_type=jnp.float32)
    block_totals = within[:, block_len - 1, :]
    strict = (jnp.arange(block_count)[:, None] > jnp.arange(block_count)[None, :]).astype(
        jnp.float32
    )
    offsets = jnp.dot(
        strict, block_totals, precision=lax.Precision.HIGHEST, preferred_element_type=jnp.float32
    )
    counts = (within + offsets[:, None, :]) * member_blocks.astype(jnp.float32)
    ranks = jnp.sum(counts, axis=2).reshape(padded_len)
    return ranks.astype(jnp.int32) - 1


def per_device(sparse_vecs, dense_vec, top_cot, top_weight, owner_ids, local_rows, table, accum):
    batch_rows, table_count, row_width = sparse_vecs.shape
    feature_count = table_count + 1
    input_cot = jnp.einsum("bh,zh->bz", top_cot, top_weight, preferred_element_type=jnp.float32)
    symmetric = jnp.dot(
        input_cot[:, row_width:],
        pair_matrix(feature_count),
        precision=lax.Precision.HIGHEST,
        preferred_element_type=jnp.float32,
    )
    symmetric = symmetric.reshape(batch_rows, feature_count, feature_count)
    features = jnp.concatenate([dense_vec[:, None, :], sparse_vecs], axis=1).astype(jnp.float32)
    feature_grad = jnp.einsum("bij,bje->bie", symmetric, features, precision=lax.Precision.HIGHEST)
    dense_grad = (input_cot[:, :row_width] + feature_grad[:, 0]).astype(jnp.bfloat16)
    sparse_grad = feature_grad[:, 1:].astype(jnp.bfloat16)
    dp_count = lax.axis_size("dp")
    rows_own = table.shape[1]
    own_cols = table_count * rows_own
    lookups = batch_rows * table_count
    capacity = 2 * lookups // dp_count
    slot_total = dp_count * capacity
    target = owner_ids.reshape(lookups)
    table_pos = jnp.arange(table_count, dtype=jnp.int32)[None, :]
    column = (
        local_rows // rows_own * own_cols + table_pos * rows_own + local_rows % rows_own
    ).reshape(lookups)
    slot_index = target * capacity + slot_ranks(target, dp_count)
    source_of = (
        jnp.full((slot_total,), -1, jnp.int32)
        .at[slot_index]
        .set(jnp.arange(lookups, dtype=jnp.int32))
    )
    filled = source_of >= 0
    safe_source = jnp.maximum(source_of, 0)
    send_rows = jnp.take(sparse_grad.reshape(lookups, row_width), safe_source, axis=0)
    send_rows = jnp.where(filled[:, None], send_rows, jnp.zeros_like(send_rows))
    send_keys = jnp.where(filled, jnp.take(column, safe_source, axis=0), -1)
    send_rows = send_rows.reshape(dp_count, capacity, row_width)
    send_keys = send_keys.reshape(dp_count, capacity)
    recv_rows, recv_keys = (
        lax.all_to_all(send_rows, "dp", split_axis=0, concat_axis=0, tiled=True),
        lax.all_to_all(send_keys, "dp", split_axis=0, concat_axis=0, tiled=True),
    )
    row_grad = sent_and_summed(
        accumulate(recv_rows, recv_keys, jnp.int32(0), own_cols * lax.axis_size("mp")).astype(
            jnp.bfloat16
        ),
        "mp",
        0,
    )
    row_grad = row_grad.reshape(table_count, rows_own, row_width)
    new_accum = accum + jnp.mean(row_grad * row_grad, axis=-1)
    new_table = table - LEARN_RATE * row_grad / (jnp.sqrt(new_accum)[:, :, None] + EPSILON)
    return (dense_grad, new_table, new_accum)


def solution(mesh):
    in_specs = (
        P(("dp", "mp"), None, None),
        P(("dp", "mp"), None),
        P(("dp", "mp"), None),
        P(),
        P(("dp", "mp"), None, None),
        P(("dp", "mp"), None),
        P(None, ("dp", "mp"), None),
        P(None, ("dp", "mp")),
    )
    out_specs = (P(("dp", "mp"), None), P(None, ("dp", "mp"), None), P(None, ("dp", "mp")))
    return jax.shard_map(
        per_device, mesh=mesh, in_specs=in_specs, out_specs=out_specs, check_vma=False
    )
```

profile of v0, /device:TPU:7, one launch (start us, length us, event | category | flops | bytes accessed | tf_op | source)
XLA Modules:
  0.0 358.9 jit_solution(17388065813966428773)
XLA Ops:
  0.7 0.8 broadcast_multiply_fusion.1
  1.5 0.9 copy.29
  2.4 0.8 fusion.23
  3.9 0.7 fusion.14
  5.0 0.5 multiply_reduce_fusion
  5.7 24.9 %scatter_custom_fusion = s32[13312]{0:T(1024)S(1)} fusion(s32[6656]{0:T(1024)S(1)} %fusion.28, s32[6656]{0:T(1024)S(1)} %iota.39, s32[]{:T(128)} %constant.98.clone.1), kind=kCustom, calls=%fused_computation.55 | custom fusion | bytes 53252 | tf_op jit(solution)/shard_map/scatter | solution.py:107
  30.6 73.7 %gather_fusion = s32[13312]{0:T(1024)S(1)} fusion(s32[6656]{0:T(1024)S(1)} %reshape.124, s32[13312]{0:T(1024)S(1)} %maximum_clamp_fusion), kind=kCustom, calls=%fused_computation | custom fusion | bytes 159744 | tf_op jit(solution)/shard_map/jit(_take)/gather | solution.py:113
  104.3 0.8 all_to_all.12
  105.1 12.5 %all-to-all-start = ((s32[64,1,208]{2,1,0:T(1,128)}), s32[64,1,208]{2,1,0:T(1,128)S(1)}, u32[]{:S(2)}, u32[]{:S(2)}) async-start(s32[64,1,208]{2,1,0:T(1,128)} %all_to_all.12), calls=%async_computation | async-start | bytes 131072 | tf_op jit(solution)/shard_map/all_to_all | solution.py:118
  118.0 3.3 fusion.18
  121.4 4.4 %copy.26 = f32[256,27,27]{2,1,0:T(8,128)} copy(f32[256,27,27]{0,2,1:T(8,128)S(1)} %reshape.123) | data formatting | bytes 1492992 | tf_op jit(solution)/shard_map/reshape | solution.py:87
  125.9 2.6 copy.25
  128.6 4.5 %fusion.8 = f32[256,27,128]{2,1,0:T(8,128)S(1)} fusion(f32[256,27,27]{2,1,0:T(8,128)} %copy.26, bf16[256,26,128]{2,1,0:T(8,128)(2,1)S(1)} %copy.25, bf16[256,1,128]{2,1,0:T(2,128)(2,1)S(1)} %copy.24), kind=kOutput, calls=%fused_computation.14 | convolution fusion | flops 290193408 | bytes 6054912 | tf_op jit(solution)/shard_map/bij,bje->bie/dot_general | solution.py:89
  133.1 1.9 copy-done.1
  135.0 1.9 slice.37
  136.9 2.6 reshape.126
  139.5 46.8 %gather_fusion.1 = bf16[13312,128]{1,0:T(8,128)(2,1)} fusion(bf16[6656,128]{1,0:T(8,128)(2,1)S(1)} %reshape.126, s32[13312]{0:T(1024)S(1)} %maximum_clamp_fusion), kind=kCustom, calls=%fused_computation.1 | custom fusion | bytes 6868992 | tf_op jit(solution)/shard_map/jit(_take)/gather | solution.py:111
  186.5 7.2 %select_select_fusion = bf16[64,208,128]{2,1,0:T(8,128)(2,1)} fusion(bf16[64,208,128]{2,1,0:T(8,128)(2,1)} %bitcast.33, pred[64,208]{1,0:T(8,128)(4,1)S(1)} %broadcast_in_dim.65, pred[64,208]{1,0:T(8,128)(4,1)S(1)} %broadcast_in_dim.63), kind=kLoop, calls=%fused_computation.13 | loop fusion | flops 3407872 | bytes 6842368 | tf_op jit(solution)/shard_map/jit(_where)/select_n | solution.py:112
  193.7 10.5 %all-to-all-start.1 = ((bf16[64,208,128]{2,1,0:T(8,128)(2,1)}), bf16[64,208,128]{2,1,0:T(8,128)(2,1)}, u32[]{:S(2)}, u32[]{:S(2)}) async-start(bf16[64,208,128]{2,1,0:T(8,128)(2,1)} %select_select_fusion), calls=%async_computation.1 | async-start | bytes 6815744 | tf_op jit(solution)/shard_map/all_to_all | solution.py:117
  204.5 78.6 %all-to-all-done.1 = bf16[64,208,128]{2,1,0:T(8,128)(2,1)} async-done(((bf16[64,208,128]{2,1,0:T(8,128)(2,1)}), bf16[64,208,128]{2,1,0:T(8,128)(2,1)}, u32[]{:S(2)}, u32[]{:S(2)}) %all-to-all-start.1) | async-done | bytes 3407904 | tf_op jit(solution)/shard_map/all_to_all | solution.py:117
  283.1 56.1 %while.14 = (s32[]{:T(128)}, f32[3328,128]{1,0:T(8,128)S(1)}, s32[4,3328]{1,0:T(4,128)S(1)}, bf16[4,3328,128]{2,1,0:T(8,128)(2,1)}, s32[]{:T(128)}, /*index=5*/s32[]{:T(128)}) while((s32[]{:T(128)}, f32[3328,128]{1,0:T(8,128)S(1)}, s32[4,3328]{1,0:T(4,128)S(1)}, bf16[4,3328,128]{2,1,0:T(8,128)(2,1)}, s32[]{:T(128)}, ...), condition=%wide.region_3.4_spmd.clone, body=%wide.region_2.3_spmd.clone.sunk | while | flops 2847277056 | bytes 4299871 | solution.py:50
  283.2 14.0 %fusion.42 = f32[3328,128]{1,0:T(8,128)S(1)} fusion(s32[3328]{0:T(1024)S(1)} %dynamic-slice_reduce_fusion.2, f32[3328,128]{1,0:T(8,128)S(1)} %get-tuple-element.171, bf16[4,3328,128]{2,1,0:T(8,128)(2,1)} %get-tuple-element.179, s32[]{:T(128)S(6)} %copy.36, pred[]{:T(512)S(6)} %compare.6), kind=kOutput, calls=%fused_computation.7.clone.1 | convolution fusion | flops 2847277056 | bytes 4273157 | tf_op jit(solution)/shard_map/while/body/eval_jaxpr/dot_general | solution.py:46
  297.2 14.0 %fusion.42 = f32[3328,128]{1,0:T(8,128)S(1)} fusion(s32[3328]{0:T(1024)S(1)} %dynamic-slice_reduce_fusion.2, f32[3328,128]{1,0:T(8,128)S(1)} %get-tuple-element.171, bf16[4,3328,128]{2,1,0:T(8,128)(2,1)} %get-tuple-element.179, s32[]{:T(128)S(6)} %copy.36, pred[]{:T(512)S(6)} %compare.6), kind=kOutput, calls=%fused_computation.7.clone.1 | convolution fusion | flops 2847277056 | bytes 4273157 | tf_op jit(solution)/shard_map/while/body/eval_jaxpr/dot_general | solution.py:46
  311.2 14.0 %fusion.42 = f32[3328,128]{1,0:T(8,128)S(1)} fusion(s32[3328]{0:T(1024)S(1)} %dynamic-slice_reduce_fusion.2, f32[3328,128]{1,0:T(8,128)S(1)} %get-tuple-element.171, bf16[4,3328,128]{2,1,0:T(8,128)(2,1)} %get-tuple-element.179, s32[]{:T(128)S(6)} %copy.36, pred[]{:T(512)S(6)} %compare.6), kind=kOutput, calls=%fused_computation.7.clone.1 | convolution fusion | flops 2847277056 | bytes 4273157 | tf_op jit(solution)/shard_map/while/body/eval_jaxpr/dot_general | solution.py:46
  325.3 14.0 %fusion.42 = f32[3328,128]{1,0:T(8,128)S(1)} fusion(s32[3328]{0:T(1024)S(1)} %dynamic-slice_reduce_fusion.2, f32[3328,128]{1,0:T(8,128)S(1)} %get-tuple-element.171, bf16[4,3328,128]{2,1,0:T(8,128)(2,1)} %get-tuple-element.179, s32[]{:T(128)S(6)} %copy.36, pred[]{:T(512)S(6)} %compare.6), kind=kOutput, calls=%fused_computation.7.clone.1 | convolution fusion | flops 2847277056 | bytes 4273157 | tf_op jit(solution)/shard_map/while/body/eval_jaxpr/dot_general | solution.py:46
  339.2 1.0 convert_element_type.38
  340.2 4.3 %all-to-all-start.2 = ((bf16[4,832,128]{2,1,0:T(8,128)(2,1)}), bf16[4,832,128]{2,1,0:T(8,128)(2,1)S(1)}, u32[]{:S(2)}, u32[]{:S(2)}) async-start(bf16[4,832,128]{2,1,0:T(8,128)(2,1)} %bitcast.6), calls=%async_computation.2 | async-start | bytes 1703936 | tf_op jit(solution)/shard_map/all_to_all | solution.py:18
  344.5 1.3 slice.27
  346.0 0.7 copy.31
  346.7 10.3 %all-to-all-done.2 = bf16[4,832,128]{2,1,0:T(8,128)(2,1)S(1)} async-done(((bf16[4,832,128]{2,1,0:T(8,128)(2,1)}), bf16[4,832,128]{2,1,0:T(8,128)(2,1)S(1)}, u32[]{:S(2)}, u32[]{:S(2)}) %all-to-all-start.2) | async-done | bytes 852000 | tf_op jit(solution)/shard_map/all_to_all | solution.py:18
  357.4 0.6 sqrt_add_fusion
  358.0 0.9 divide_subtract_fusion
  (44 shorter events, 3.2 us)
Async XLA Ops:
  0.6 116.9 %copy-start = (bf16[479,1024]{1,0:T(8,128)(2,1)S(1)}, bf16[479,1024]{1,0:T(8,128)(2,1)}, u32[]{:S(2)}) copy-start(bf16[479,1024]{1,0:T(8,128)(2,1)} %param.14) | copy-start | bytes 2942980
  30.6 87.0 %copy-start.2 = (bf16[256,1024]{1,0:T(8,128)(2,1)S(1)}, bf16[256,1024]{1,0:T(8,128)(2,1)}, u32[]{:S(2)}) copy-start(bf16[256,1024]{1,0:T(8,128)(2,1)} %param.13) | copy-start | bytes 1572868
  105.1 88.6 %all-to-all-start = ((s32[64,1,208]{2,1,0:T(1,128)}), s32[64,1,208]{2,1,0:T(1,128)S(1)}, u32[]{:S(2)}, u32[]{:S(2)}) async-start(s32[64,1,208]{2,1,0:T(1,128)} %all_to_all.12), calls=%async_computation | async-start | bytes 131072 | tf_op jit(solution)/shard_map/all_to_all | solution.py:118
  125.9 2.6 copy-start.4
  133.1 1.9 copy-start.1
  193.7 89.4 %all-to-all-start.1 = ((bf16[64,208,128]{2,1,0:T(8,128)(2,1)}), bf16[64,208,128]{2,1,0:T(8,128)(2,1)}, u32[]{:S(2)}, u32[]{:S(2)}) async-start(bf16[64,208,128]{2,1,0:T(8,128)(2,1)} %select_select_fusion), calls=%async_computation.1 | async-start | bytes 6815744 | tf_op jit(solution)/shard_map/all_to_all | solution.py:117
  340.2 17.2 %copy-start.5 = (f32[26,32]{1,0:T(8,128)S(1)}, f32[26,32]{1,0:T(8,128)}, u32[]{:S(2)}) copy-start(f32[26,32]{1,0:T(8,128)} %param.18) | copy-start | bytes 9988
  340.2 17.8 %copy-start.3 = (f32[26,32,128]{2,1,0:T(8,128)S(1)}, f32[26,32,128]{2,1,0:T(8,128)}, u32[]{:S(2)}) copy-start(f32[26,32,128]{2,1,0:T(8,128)} %param.17) | copy-start | bytes 1277956
  340.2 16.7 %all-to-all-start.2 = ((bf16[4,832,128]{2,1,0:T(8,128)(2,1)}), bf16[4,832,128]{2,1,0:T(8,128)(2,1)S(1)}, u32[]{:S(2)}, u32[]{:S(2)}) async-start(bf16[4,832,128]{2,1,0:T(8,128)(2,1)} %bitcast.6), calls=%async_computation.2 | async-start | bytes 1703936 | tf_op jit(solution)/shard_map/all_to_all | solution.py:18
where the time goes:
time: 360 us; the launch traced here: 359 us
  local copies, waits for them, and re-layouts  164 us (46%)
  waiting for transfers between devices  88.9 us (25%)
  matrix products  64.8 us (18%)
  starting transfers between devices  27.3 us (8%)
  other arithmetic  12.6 us (4%)
    all_to_all x1, waiting for transfers between devices, per_device(): lax.all_to_all(send_rows, 'dp', split_axis=0, concat_axis=0, tiled=True)  78.6 us
    gather x1, local copies, waits for them, and re-layouts, per_device(): send_keys = jnp.where(filled, jnp.take(column, safe_source, axis=0), -1)  73.7 us
    dot_general x4, matrix products, add_block(): lax.dot_general(onehot, row_piece, (((0,), (0,)), ((), ())), preferred_el...  55.8 us
    gather x1, local copies, waits for them, and re-layouts, per_device(): jnp.take(sparse_grad.reshape(lookups, row_width), safe_source, axis=0)  46.8 us
    scatter x1, local copies, waits for them, and re-layouts, per_device(): source_of = jnp.full((slot_total,), -1, jnp.int32).at[slot_index].set(jnp...  24.9 us
    all_to_all x1, starting transfers between devices, per_device(): lax.all_to_all(send_keys, 'dp', split_axis=0, concat_axis=0, tiled=True)  12.5 us
    all_to_all x1, starting transfers between devices, per_device(): lax.all_to_all(send_rows, 'dp', split_axis=0, concat_axis=0, tiled=True)  10.5 us
    all_to_all x1, waiting for transfers between devices, sent_and_summed(): lax.all_to_all(pieces, axis, split_axis=0, concat_axis=0, tiled=True)  10.3 us
  transfers between devices with their start and end apart: 3, of which 2 were waited for; matrix products, arithmetic and copies ran while one was open for 21% of the time, Pallas kernels for 0%

commit v1 on v0

v1 whole, which is shorter than its diff:
```python
import jax
import jax.numpy as jnp
from jax import lax
from jax.experimental import pallas as pl
from jax.experimental.pallas import tpu as pltpu
from jax.sharding import PartitionSpec as P

LEARN_RATE = 0.1
EPSILON = 1e-08

MESH = pl.DeviceIdType.MESH
BF16 = jnp.bfloat16
F32 = jnp.float32
I32 = jnp.int32

BATCH = 256
TABLES = 26
FEATS = 27
WIDTH = 128
GROUP = 8
GROUPS = BATCH // GROUP
ITEMS = TABLES * GROUP
LOOKUPS = BATCH * TABLES
CAP = 208
RANKS = 256
OWNERS = 64
PIECE = 832
PIECES = 4
PLANE = 32
SLOTS = 2 * PLANE


def prepare_kernel(comb_ref, sparse_ref, dense_ref, cot_ref, weight_ref, grad_ref, dgrad_ref, src_ref, key_ref,
                   member_ref, cum_ref, sym_ref, ic_ref):
    sample = lax.broadcasted_iota(I32, (1, BATCH), 1)
    upto = (lax.broadcasted_iota(I32, (BATCH, BATCH), 0) <= lax.broadcasted_iota(I32, (BATCH, BATCH), 1)).astype(F32).astype(BF16)
    owner_row = lax.broadcasted_iota(I32, (OWNERS, BATCH), 0)
    for t in range(TABLES):
        own = lax.shift_right_logical(comb_ref[t : t + 1, :], 7)
        member_ref[t * OWNERS : (t + 1) * OWNERS, :] = (own == owner_row).astype(F32).astype(BF16)
    cum_ref[...] = jnp.dot(member_ref[...], upto, preferred_element_type=F32)
    group_of = (lax.shift_right_logical(sample, 3) + 1).astype(F32)
    rank_row = lax.broadcasted_iota(I32, (RANKS, BATCH), 0)
    carry = jnp.zeros((OWNERS, 1), F32)
    found = jnp.zeros((3 * OWNERS, RANKS), F32)
    for t in range(TABLES):
        member = member_ref[t * OWNERS : (t + 1) * OWNERS, :].astype(F32)
        count = cum_ref[t * OWNERS : (t + 1) * OWNERS, :] + carry
        rank = jnp.sum(member * count, axis=0, keepdims=True).astype(I32) - 1
        carry = count[:, BATCH - 1 : BATCH]
        at_rank = (rank == rank_row).astype(F32).astype(BF16)
        row = (comb_ref[t : t + 1, :] & 127).astype(F32)
        place = (t * GROUP + (sample & 7)).astype(F32)
        values = jnp.concatenate([member * group_of, member * place, member * row], axis=0).astype(BF16)
        found = found + lax.dot_general(values, at_rank, (((1,), (1,)), ((), ())), preferred_element_type=F32)
    found = found.astype(I32)
    group, place, row = found[:OWNERS], found[OWNERS : 2 * OWNERS], found[2 * OWNERS :]
    src_ref[...] = jnp.where(group > 0, (group - 1) * ITEMS + place, LOOKUPS)
    key_ref[...] = lax.shift_right_logical(row, 5) * PIECE + lax.shift_right_logical(place, 3) * 32 + (row & 31)

    ic = lax.dot_general(cot_ref[...], weight_ref[...], (((1,), (1,)), ((), ())), preferred_element_type=F32)
    ic_ref[...] = ic[:, :WIDTH]
    pairs = ic[:, WIDTH:].astype(BF16)
    pair_count = pairs.shape[1]
    pair_row = lax.broadcasted_iota(I32, (pair_count, 256), 0)
    lane = lax.broadcasted_iota(I32, (1, 256), 1)
    col = lane & 31
    other = jnp.where(col == FEATS - 1, 0, col + 1)
    own_sample = (lax.broadcasted_iota(I32, (GROUP, 256), 0) == lax.shift_right_logical(lax.broadcasted_iota(I32, (GROUP, 256), 1), 5))[None]

    def spread(f):
        if f >= FEATS:
            return jnp.zeros((GROUPS, GROUP, 256), F32)
        this = (f + 1) % FEATS
        low, high = jnp.minimum(other, this), jnp.maximum(other, this)
        pair = lax.shift_right_logical(high * (high - 1), 1) + low
        pair = jnp.where((col < FEATS) & (other != this), pair, -1)
        place = (pair_row == pair).astype(F32).astype(BF16)
        wide = jnp.dot(pairs, place, preferred_element_type=F32).reshape(GROUPS, GROUP, 256)
        return jnp.where(own_sample, wide, 0.0)

    for f in range(0, FEATS + 1, 2):
        sym_ref[:, f * GROUP : (f + 2) * GROUP, :] = jnp.concatenate([spread(f), spread(f + 1)], axis=1).astype(BF16)

    def one_group(g, _):
        first = pl.multiple_of(g * GROUP, GROUP)
        feats = jnp.concatenate(
            [sparse_ref[pl.ds(first, GROUP)], dense_ref[pl.ds(first, GROUP), :][:, None, :], jnp.zeros((GROUP, 32 - FEATS, WIDTH), BF16)],
            axis=1,
        ).reshape(GROUP * 32, WIDTH)
        out = jnp.dot(sym_ref[g], feats, preferred_element_type=F32)
        grad_ref[pl.ds(pl.multiple_of(g * ITEMS, 8), ITEMS), :] = out[:ITEMS]
        dgrad_ref[pl.ds(first, GROUP), :] = (ic_ref[pl.ds(first, GROUP), :] + out[ITEMS : ITEMS + GROUP]).astype(BF16)
        return 0

    lax.fori_loop(0, GROUPS, one_group, 0)
    grad_ref[LOOKUPS : LOOKUPS + 8, :] = jnp.zeros((8, WIDTH), F32)


def prepare(comb, sparse_vecs, dense_vec, top_cot, top_weight):
    vmem = pl.BlockSpec(memory_space=pltpu.VMEM)
    return pl.pallas_call(
        prepare_kernel,
        out_shape=(
            jax.ShapeDtypeStruct((LOOKUPS + 8, WIDTH), F32),
            jax.ShapeDtypeStruct((BATCH, WIDTH), BF16),
            jax.ShapeDtypeStruct((OWNERS, RANKS), I32),
            jax.ShapeDtypeStruct((OWNERS, RANKS), I32),
        ),
        in_specs=[vmem] * 5,
        out_specs=(vmem,) * 4,
        scratch_shapes=[
            pltpu.VMEM((TABLES * OWNERS, BATCH), BF16),
            pltpu.VMEM((TABLES * OWNERS, BATCH), F32),
            pltpu.VMEM((GROUPS, (FEATS + 1) * GROUP, 256), BF16),
            pltpu.VMEM((BATCH, WIDTH), F32),
        ],
        name="prepare",
    )(comb, sparse_vecs, dense_vec, top_cot, top_weight)


def shift_of(y, z, half):
    quarter = lax.rem(z - half - jnp.where(y == 3, 2, 0) + 8, 4)
    odd = jnp.where(quarter == 0, -1, jnp.where(quarter == 1, 1, jnp.where(quarter == 2, 3, -3)))
    even = jnp.where(y == 0, 4 * lax.rem(half + z // 2, 2), 2 - 4 * lax.rem(half + z, 2))
    return jnp.where(lax.rem(y, 2) == 1, odd, even)


def exchange_kernel(grad_ref, src_ref, key_ref, out_ref, rows_out, rows_in, keys_in, block, acc, piece_out, piece_in,
                    row_send, row_recv, key_send, key_recv, piece_send, piece_recv):
    dp, y = lax.axis_index("dp"), lax.axis_index("mp")
    x, z, core = dp // 16, lax.rem(dp // 2, 8), lax.rem(dp, 2)

    def dp_of(x, z, core):
        return x * 16 + z * 2 + core

    def peer(step):
        mixed = lax.rem(step * 5, PLANE)
        px, py = lax.rem(x + mixed // 8, 4), lax.rem(y + lax.rem(mixed // 2, 4), 4)
        return px, py, lax.rem(core + mixed, 2)

    def target(half):
        return lax.rem(z + shift_of(y, z, half) + 8, 8)

    barrier = pltpu.get_barrier_semaphore()

    def greet_plane(step, _):
        mixed = lax.rem(step * 5, PLANE)
        px, py = lax.rem(x - mixed // 8 + 4, 4), lax.rem(y - lax.rem(mixed // 2, 4) + 4, 4)
        pl.semaphore_signal(barrier, inc=1, device_id=(dp_of(px, z, lax.rem(core + mixed, 2)), py), device_id_type=MESH)
        return 0

    lax.fori_loop(1, PLANE, greet_plane, 0)

    def greet_source(zs, _):
        away = lax.rem(z - zs + 8, 8)
        quarter = jnp.where(away == 7, 0, jnp.where(away == 1, 1, jnp.where(away == 3, 2, 3)))
        ys = jnp.where(lax.rem(away, 4) == 0, 0, jnp.where(lax.rem(away, 2) == 0, 2, jnp.where(lax.rem(zs - quarter + 8, 4) < 2, 1, 3)))

        @pl.when((zs != z) | (ys != y))
        def _():
            pl.semaphore_signal(barrier, inc=1, device_id=(dp_of(x, zs, core), ys), device_id_type=MESH)

        return 0

    lax.fori_loop(0, 8, greet_source, 0)
    pl.semaphore_wait(barrier, PLANE - 1 + 8 - jnp.where(y == 0, 1, 0))

    def owner_of(step, half):
        px, py, pcore = peer(step)
        return dp_of(px, lax.rem(z + shift_of(py, z, half) + 8, 8), pcore)

    def key_copy(slot, owner, device):
        return pltpu.make_async_remote_copy(
            src_ref=key_ref.at[owner], dst_ref=keys_in.at[slot], send_sem=key_send, recv_sem=key_recv, device_id=device, device_id_type=MESH
        )

    def send_keys(slot, _):
        half, step = slot // PLANE, lax.rem(slot, PLANE)
        owner = owner_of(step, half)
        px, py, pcore = peer(step)

        @pl.when(step == 0)
        def _():
            pltpu.make_async_copy(key_ref.at[owner], keys_in.at[slot], key_recv).start()

        @pl.when(step != 0)
        def _():
            key_copy(slot, owner, (dp_of(px, z, pcore), py)).start()

        return 0

    lax.fori_loop(0, SLOTS, send_keys, 0)

    def send_rows(slot, _):
        half, step = slot // PLANE, lax.rem(slot, PLANE)
        owner = owner_of(step, half)
        px, py, pcore = peer(step)

        def gather(r, _):
            for k in range(16):
                at = r * 16 + k
                block[pl.ds(at, 1), :] = grad_ref[pl.ds(src_ref[owner, at], 1), :]
            return 0

        lax.fori_loop(0, CAP // 16, gather, 0)

        @pl.when(step == 0)
        def _():
            rows_in[slot] = block[...].astype(BF16)

        @pl.when(step != 0)
        def _():
            rows_out[slot] = block[...].astype(BF16)
            pltpu.make_async_remote_copy(
                src_ref=rows_out.at[slot],
                dst_ref=rows_in.at[slot],
                send_sem=row_send,
                recv_sem=row_recv.at[slot],
                device_id=(dp_of(px, z, pcore), py),
                device_id_type=MESH,
            ).start()

        return 0

    lax.fori_loop(0, SLOTS, send_rows, 0)

    pltpu.make_async_copy(keys_in, keys_in, key_recv).wait()

    row_of = lax.broadcasted_iota(I32, (PIECE, CAP), 0)

    def sum_half(half):
        acc[...] = jnp.zeros_like(acc)

        def add(turn, _):
            slots = [half * PLANE + turn * 4 + k for k in range(4)]
            for slot in slots:

                @pl.when(lax.rem(slot, PLANE) != 0)
                def _():
                    pltpu.make_async_copy(rows_in.at[slot], rows_in.at[slot], row_recv.at[slot]).wait()

            rows = [rows_in[slot] for slot in slots]
            keys = [keys_in[slot][:, :CAP] for slot in slots]
            for p in range(PIECES):
                total = acc[p]
                for k in range(4):
                    onehot = (row_of == keys[k] - p * PIECE).astype(F32).astype(BF16)
                    total = total + jnp.dot(onehot, rows[k], preferred_element_type=F32)
                acc[p] = total
            return 0

        lax.fori_loop(0, PLANE // 4, add, 0)

        zt = target(half)

        def send_piece(k, _):
            p = lax.rem(y + k + 1, PIECES)
            at = half * PIECES + p
            piece_out[at] = acc[p].astype(BF16)

            @pl.when((zt == z) & (p == y))
            def _():
                pltpu.make_async_copy(piece_out.at[at], piece_in.at[z], piece_recv.at[z]).start()

            @pl.when((zt != z) | (p != y))
            def _():
                pltpu.make_async_remote_copy(
                    src_ref=piece_out.at[at],
                    dst_ref=piece_in.at[z],
                    send_sem=piece_send,
                    recv_sem=piece_recv.at[z],
                    device_id=(dp_of(x, zt, core), p),
                    device_id_type=MESH,
                ).start()

            return 0

        lax.fori_loop(0, PIECES, send_piece, 0)

    sum_half(0)
    sum_half(1)

    def add_piece(zs, total):
        pltpu.make_async_copy(piece_in.at[zs], piece_in.at[zs], piece_recv.at[zs]).wait()
        return 0

    lax.fori_loop(0, 8, add_piece, 0)
    total = piece_in[0].astype(F32)
    for zs in range(1, 8):
        total = total + piece_in[zs].astype(F32)
    out_ref[...] = total

    def rows_left(slot, _):
        @pl.when(lax.rem(slot, PLANE) != 0)
        def _():
            pltpu.make_async_copy(rows_out.at[slot], rows_out.at[slot], row_send).wait()
            pltpu.make_async_copy(key_ref.at[0], key_ref.at[0], key_send).wait()

        return 0

    lax.fori_loop(0, SLOTS, rows_left, 0)

    def piece_left(k, _):
        pltpu.make_async_copy(piece_out.at[0], piece_out.at[0], piece_send).wait()
        return 0

    lax.fori_loop(0, 2 * PIECES - jnp.where(y == 0, 1, 0), piece_left, 0)


def exchange(grad, src, key):
    vmem = pl.BlockSpec(memory_space=pltpu.VMEM)
    return pl.pallas_call(
        exchange_kernel,
        out_shape=jax.ShapeDtypeStruct((PIECE, WIDTH), F32),
        in_specs=[vmem, pl.BlockSpec(memory_space=pltpu.SMEM), vmem],
        out_specs=vmem,
        scratch_shapes=[
            pltpu.VMEM((SLOTS, CAP, WIDTH), BF16),
            pltpu.VMEM((SLOTS, CAP, WIDTH), BF16),
            pltpu.VMEM((SLOTS, 1, RANKS), I32),
            pltpu.VMEM((CAP, WIDTH), F32),
            pltpu.VMEM((PIECES, PIECE, WIDTH), F32),
            pltpu.VMEM((2 * PIECES, PIECE, WIDTH), BF16),
            pltpu.VMEM((8, PIECE, WIDTH), BF16),
            pltpu.SemaphoreType.DMA,
            pltpu.SemaphoreType.DMA((SLOTS,)),
            pltpu.SemaphoreType.DMA,
            pltpu.SemaphoreType.DMA,
            pltpu.SemaphoreType.DMA,
            pltpu.SemaphoreType.DMA((8,)),
        ],
        compiler_params=pltpu.CompilerParams(collective_id=0, has_side_effects=True),
        name="exchange",
    )(grad, src, key.reshape(OWNERS, 1, RANKS))


def per_device(sparse_vecs, dense_vec, top_cot, top_weight, owner_ids, local_rows, table, accum):
    comb = (owner_ids[:, :, 0] * 128 + local_rows).T
    grad, dense_grad, src, key = prepare(comb, sparse_vecs, dense_vec, top_cot, top_weight)
    row_grad = exchange(grad, src, key).reshape(table.shape)
    new_accum = accum + jnp.mean(row_grad * row_grad, axis=-1)
    new_table = table - LEARN_RATE * row_grad / (jnp.sqrt(new_accum)[:, :, None] + EPSILON)
    return (dense_grad, new_table, new_accum)


def solution(mesh):
    in_specs = (
        P(("dp", "mp"), None, None),
        P(("dp", "mp"), None),
        P(("dp", "mp"), None),
        P(),
        P(("dp", "mp"), None, None),
        P(("dp", "mp"), None),
        P(None, ("dp", "mp"), None),
        P(None, ("dp", "mp")),
    )
    out_specs = (P(("dp", "mp"), None), P(None, ("dp", "mp"), None), P(None, ("dp", "mp")))
    return jax.shard_map(
        per_device, mesh=mesh, in_specs=in_specs, out_specs=out_specs, check_vma=False
    )
```

time: 360 us -> 141 us (0.39)
  local copies, waits for them, and re-layouts: 164 us -> 5.55 us
  Pallas kernels: 0 us -> 130 us
  waiting for transfers between devices: 88.9 us -> 0 us
  matrix products: 64.8 us -> 0 us
  starting transfers between devices: 27.3 us -> 0 us
  other arithmetic: 12.6 us -> 4.15 us
    pallas_call x0 -> x2, Pallas kernels: none -> 130 us  [the longest x1 117 us: exchange(): pl.pallas_call(exchange_kernel, out_shape=jax.ShapeDtypeStruct((PIECE, WI...]
    gather x2 -> x0, local copies, waits for them, and re-layouts: 120 us -> none  [the longest x1 73.7 us: per_device(): send_keys = jnp.where(filled, jnp.take(column, safe_source, axis=0), -1)]
    all_to_all x3 -> x0, waiting for transfers between devices: 88.9 us -> none  [the longest x1 78.6 us: per_device(): lax.all_to_all(send_rows, 'dp', split_axis=0, concat_axis=0, tiled=True)]
    dot_general x9 -> x0, matrix products: 64.8 us -> none  [the longest x4 55.8 us: add_block(): lax.dot_general(onehot, row_piece, (((0,), (0,)), ((), ())), preferred_el...]
    all_to_all x3 -> x0, starting transfers between devices: 27.3 us -> none  [the longest x1 12.5 us: per_device(): lax.all_to_all(send_keys, 'dp', split_axis=0, concat_axis=0, tiled=True)]
    scatter x1 -> x0, local copies, waits for them, and re-layouts: 24.9 us -> none  [per_device(): source_of = jnp.full((slot_total,), -1, jnp.int32).at[slot_index].set(jnp...]
    select_n x3 -> x0, other arithmetic: 7.36 us -> none  [the longest x1 7.24 us: per_device(): send_rows = jnp.where(filled[:, None], send_rows, jnp.zeros_like(send_rows))]
    reshape x5 -> x1, local copies, waits for them, and re-layouts: 7.35 us -> 1.51 us  [exchange(): key.reshape(OWNERS, 1, RANKS)]
  transfers between devices with their start and end apart: 3 -> 0, of which waited for: 2 -> 0; matrix products, arithmetic and copies ran while one was open for 21% -> 0% of each run, Pallas kernels for 0% -> 0%
where the time goes in v1:
time: 141 us; the launch traced here: 140 us
  Pallas kernels  130 us (92%)
  local copies, waits for them, and re-layouts  5.55 us (4%)
  other arithmetic  4.15 us (3%)
    pallas_call x1, Pallas kernels, exchange(): pl.pallas_call(exchange_kernel, out_shape=jax.ShapeDtypeStruct((PIECE, WI...  117 us
    pallas_call x1, Pallas kernels, prepare(): pl.pallas_call(prepare_kernel, out_shape=(jax.ShapeDtypeStruct((LOOKUPS +...  13.4 us
    unnamed x5, local copies, waits for them, and re-layouts  3.97 us

profile of v1, /device:TPU:7, one launch (start us, length us, event | category | flops | bytes accessed | tf_op | source)
XLA Modules:
  0.0 140.3 jit_solution(3135765811077214640)
XLA Ops:
  0.6 1.4 fusion.comb_ref
  2.0 4.0 %copy.12.sparse_ref = bf16[256,26,128]{2,1,0:T(8,128)(2,1)} copy(bf16[256,26,128]{2,0,1:T(8,128)(2,1)} %param.8) | data formatting | bytes 3407872 | tf_op args[0]
  6.0 13.4 %prepare.1 = (f32[6664,128]{1,0:T(8,128)}, bf16[256,128]{1,0:T(8,128)(2,1)}, s32[64,256]{1,0:T(8,128)}, s32[64,256]{1,0:T(8,128)}) custom-call(s32[26,256]{1,0:T(8,128)} %fusion.comb_ref, bf16[256,26,128]{2,1,0:T(8,128)(2,1)} %copy.12.sparse_ref, bf16[256,128]{1,0:T(8,128)(2,1)} %dense_ref.1, bf16[256,1024]{1,0:T(8,128)(2,1)} %cot_ref.1, ...), custom_call_target="tpu_custom_call" | custom-call | tf_op jit(solution)/shard_map/prepare/pallas_call | solution.py:102
  19.4 1.5 %reshape.19.key_ref = s32[64,1,256]{2,1,0:T(1,128)} reshape(s32[64,256]{1,0:T(8,128)} %get-tuple-element.10) | data formatting | bytes 131072 | tf_op jit(solution)/shard_map/reshape | solution.py:335
  20.9 0.0 copy-start.1
  20.9 0.0 copy-start
  20.9 116.5 %exchange.1 = f32[832,128]{1,0:T(8,128)} custom-call(f32[6664,128]{1,0:T(8,128)} %get-tuple-element.8.grad_ref, s32[64,256]{1,0:T(8,128)} %get-tuple-element.9.src_ref, s32[64,1,256]{2,1,0:T(1,128)} %reshape.19.key_ref), custom_call_target="tpu_custom_call" | custom-call | tf_op jit(solution)/shard_map/exchange/pallas_call | solution.py:313
  137.4 1.2 multiply_reduce_fusion
  138.6 0.1 div.18
  138.7 0.0 copy-done.1
  138.7 0.6 sqrt_add_fusion
  139.3 0.0 copy-done
  139.3 0.9 divide_subtract_fusion
  (1 shorter events, 0.0 us)
Async XLA Ops:
  20.9 117.8 %copy-start.1 = (f32[26,32]{1,0:T(8,128)S(1)}, f32[26,32]{1,0:T(8,128)}, u32[]{:S(2)}) copy-start(f32[26,32]{1,0:T(8,128)} %param.15) | copy-start | bytes 9988
  20.9 118.4 %copy-start = (f32[26,32,128]{2,1,0:T(8,128)S(1)}, f32[26,32,128]{2,1,0:T(8,128)}, u32[]{:S(2)}) copy-start(f32[26,32,128]{2,1,0:T(8,128)} %param.14) | copy-start | bytes 1277956

commit v2 on v1

--- a/solution.py
+++ b/solution.py
@@ -30,13 +30,13 @@
 SLOTS = 2 * PLANE
 
 
-def prepare_kernel(comb_ref, sparse_ref, dense_ref, cot_ref, weight_ref, grad_ref, dgrad_ref, src_ref, key_ref,
+def prepare_kernel(owner_ref, local_ref, sparse_ref, dense_ref, cot_ref, weight_ref, grad_ref, dgrad_ref, src_ref, key_ref,
                    member_ref, cum_ref, sym_ref, ic_ref):
     sample = lax.broadcasted_iota(I32, (1, BATCH), 1)
     upto = (lax.broadcasted_iota(I32, (BATCH, BATCH), 0) <= lax.broadcasted_iota(I32, (BATCH, BATCH), 1)).astype(F32).astype(BF16)
     owner_row = lax.broadcasted_iota(I32, (OWNERS, BATCH), 0)
     for t in range(TABLES):
-        own = lax.shift_right_logical(comb_ref[t : t + 1, :], 7)
+        own = owner_ref[t]
         member_ref[t * OWNERS : (t + 1) * OWNERS, :] = (own == owner_row).astype(F32).astype(BF16)
     cum_ref[...] = jnp.dot(member_ref[...], upto, preferred_element_type=F32)
     group_of = (lax.shift_right_logical(sample, 3) + 1).astype(F32)
@@ -49,14 +49,15 @@
         rank = jnp.sum(member * count, axis=0, keepdims=True).astype(I32) - 1
         carry = count[:, BATCH - 1 : BATCH]
         at_rank = (rank == rank_row).astype(F32).astype(BF16)
-        row = (comb_ref[t : t + 1, :] & 127).astype(F32)
+        row = local_ref[t : t + 1, :].astype(F32)
         place = (t * GROUP + (sample & 7)).astype(F32)
         values = jnp.concatenate([member * group_of, member * place, member * row], axis=0).astype(BF16)
         found = found + lax.dot_general(values, at_rank, (((1,), (1,)), ((), ())), preferred_element_type=F32)
     found = found.astype(I32)
     group, place, row = found[:OWNERS], found[OWNERS : 2 * OWNERS], found[2 * OWNERS :]
     src_ref[...] = jnp.where(group > 0, (group - 1) * ITEMS + place, LOOKUPS)
-    key_ref[...] = lax.shift_right_logical(row, 5) * PIECE + lax.shift_right_logical(place, 3) * 32 + (row & 31)
+    key = lax.shift_right_logical(row, 5) * PIECE + lax.shift_right_logical(place, 3) * 32 + (row & 31)
+    key_ref[...] = key[:, None, :]
 
     ic = lax.dot_general(cot_ref[...], weight_ref[...], (((1,), (1,)), ((), ())), preferred_element_type=F32)
     ic_ref[...] = ic[:, :WIDTH]
@@ -64,9 +65,9 @@
     pair_count = pairs.shape[1]
     pair_row = lax.broadcasted_iota(I32, (pair_count, 256), 0)
     lane = lax.broadcasted_iota(I32, (1, 256), 1)
-    col = lane & 31
+    col = lax.shift_right_logical(lane, 3)
     other = jnp.where(col == FEATS - 1, 0, col + 1)
-    own_sample = (lax.broadcasted_iota(I32, (GROUP, 256), 0) == lax.shift_right_logical(lax.broadcasted_iota(I32, (GROUP, 256), 1), 5))[None]
+    own_sample = (lax.broadcasted_iota(I32, (GROUP, 256), 0) == (lax.broadcasted_iota(I32, (GROUP, 256), 1) & 7))[None]
 
     def spread(f):
         if f >= FEATS:
@@ -85,8 +86,8 @@
     def one_group(g, _):
         first = pl.multiple_of(g * GROUP, GROUP)
         feats = jnp.concatenate(
-            [sparse_ref[pl.ds(first, GROUP)], dense_ref[pl.ds(first, GROUP), :][:, None, :], jnp.zeros((GROUP, 32 - FEATS, WIDTH), BF16)],
-            axis=1,
+            [sparse_ref[:, pl.ds(first, GROUP), :], dense_ref[pl.ds(first, GROUP), :][None], jnp.zeros((32 - FEATS, GROUP, WIDTH), BF16)],
+            axis=0,
         ).reshape(GROUP * 32, WIDTH)
         out = jnp.dot(sym_ref[g], feats, preferred_element_type=F32)
         grad_ref[pl.ds(pl.multiple_of(g * ITEMS, 8), ITEMS), :] = out[:ITEMS]
@@ -97,7 +98,7 @@
     grad_ref[LOOKUPS : LOOKUPS + 8, :] = jnp.zeros((8, WIDTH), F32)
 
 
-def prepare(comb, sparse_vecs, dense_vec, top_cot, top_weight):
+def prepare(owner, local, sparse_vecs, dense_vec, top_cot, top_weight):
     vmem = pl.BlockSpec(memory_space=pltpu.VMEM)
     return pl.pallas_call(
         prepare_kernel,
@@ -105,9 +106,9 @@
             jax.ShapeDtypeStruct((LOOKUPS + 8, WIDTH), F32),
             jax.ShapeDtypeStruct((BATCH, WIDTH), BF16),
             jax.ShapeDtypeStruct((OWNERS, RANKS), I32),
-            jax.ShapeDtypeStruct((OWNERS, RANKS), I32),
+            jax.ShapeDtypeStruct((OWNERS, 1, RANKS), I32),
         ),
-        in_specs=[vmem] * 5,
+        in_specs=[vmem] * 6,
         out_specs=(vmem,) * 4,
         scratch_shapes=[
             pltpu.VMEM((TABLES * OWNERS, BATCH), BF16),
@@ -116,7 +117,7 @@
             pltpu.VMEM((BATCH, WIDTH), F32),
         ],
         name="prepare",
-    )(comb, sparse_vecs, dense_vec, top_cot, top_weight)
+    )(owner, local, sparse_vecs, dense_vec, top_cot, top_weight)
 
 
 def shift_of(y, z, half):
@@ -197,13 +198,8 @@
         owner = owner_of(step, half)
         px, py, pcore = peer(step)
 
-        def gather(r, _):
-            for k in range(16):
-                at = r * 16 + k
-                block[pl.ds(at, 1), :] = grad_ref[pl.ds(src_ref[owner, at], 1), :]
-            return 0
-
-        lax.fori_loop(0, CAP // 16, gather, 0)
+        for rank in range(CAP):
+            block[rank : rank + 1, :] = grad_ref[pl.ds(src_ref[owner, rank], 1), :]
 
         @pl.when(step == 0)
         def _():
@@ -240,14 +236,18 @@
                 def _():
                     pltpu.make_async_copy(rows_in.at[slot], rows_in.at[slot], row_recv.at[slot]).wait()
 
-            rows = [rows_in[slot] for slot in slots]
-            keys = [keys_in[slot][:, :CAP] for slot in slots]
+            total = None
+            for slot in slots:
+                key = keys_in[slot][:, :CAP]
+                piece = sum((key >= p * PIECE).astype(I32) for p in range(1, PIECES))
+                piece_col = jnp.broadcast_to(piece.astype(F32), (8, CAP)).T[:, :1]
+                rows = rows_in[slot].astype(F32)
+                wide = jnp.concatenate([jnp.where(piece_col == float(p), rows, 0.0).astype(BF16) for p in range(PIECES)], axis=1)
+                onehot = (row_of == key - piece * PIECE).astype(F32).astype(BF16)
+                part = jnp.dot(onehot, wide, preferred_element_type=F32)
+                total = part if total is None else total + part
             for p in range(PIECES):
-                total = acc[p]
-                for k in range(4):
-                    onehot = (row_of == keys[k] - p * PIECE).astype(F32).astype(BF16)
-                    total = total + jnp.dot(onehot, rows[k], preferred_element_type=F32)
-                acc[p] = total
+                acc[p] += total[:, p * WIDTH : (p + 1) * WIDTH]
             return 0
 
         lax.fori_loop(0, PLANE // 4, add, 0)
@@ -332,12 +332,13 @@
         ],
         compiler_params=pltpu.CompilerParams(collective_id=0, has_side_effects=True),
         name="exchange",
-    )(grad, src, key.reshape(OWNERS, 1, RANKS))
+    )(grad, src, key)
 
 
 def per_device(sparse_vecs, dense_vec, top_cot, top_weight, owner_ids, local_rows, table, accum):
-    comb = (owner_ids[:, :, 0] * 128 + local_rows).T
-    grad, dense_grad, src, key = prepare(comb, sparse_vecs, dense_vec, top_cot, top_weight)
+    owner = jnp.transpose(owner_ids, (1, 2, 0))
+    sparse_vecs = jnp.transpose(sparse_vecs, (1, 0, 2))
+    grad, dense_grad, src, key = prepare(owner, local_rows.T, sparse_vecs, dense_vec, top_cot, top_weight)
     row_grad = exchange(grad, src, key).reshape(table.shape)
     new_accum = accum + jnp.mean(row_grad * row_grad, axis=-1)
     new_table = table - LEARN_RATE * row_grad / (jnp.sqrt(new_accum)[:, :, None] + EPSILON)

time: 141 us -> 114 us (0.81)
  the two profiles are of different devices: /device:TPU:7 before, /device:TPU:62 now
where the time goes in v2:
time: 114 us
  Pallas kernels  111 us (97%)
  other arithmetic  2.77 us (2%)
    pallas_call x1, Pallas kernels, exchange(): pl.pallas_call(exchange_kernel, out_shape=jax.ShapeDtypeStruct((PIECE, WI...  97.4 us
    pallas_call x1, Pallas kernels, prepare(): pl.pallas_call(prepare_kernel, out_shape=(jax.ShapeDtypeStruct((LOOKUPS +...  13.3 us

profile of v2, /device:TPU:62, one launch (start us, length us, event | category | flops | bytes accessed | tf_op | source)
XLA Modules:
  0.0 114.2 jit_solution(8647121826873676250)
XLA Ops:
  0.6 0.0 copy-start.1
  0.6 0.0 copy-start
  0.7 13.3 %prepare.1 = (f32[6664,128]{1,0:T(8,128)}, bf16[256,128]{1,0:T(8,128)(2,1)}, s32[64,256]{1,0:T(8,128)}, s32[64,1,256]{2,1,0:T(1,128)}) custom-call(s32[26,1,256]{2,1,0:T(1,128)} %bitcast.7, s32[26,256]{1,0:T(8,128)} %bitcast.6, bf16[26,256,128]{2,1,0:T(8,128)(2,1)} %bitcast.5, bf16[256,128]{1,0:T(8,128)(2,1)} %dense_ref.1, bf16[256,1024]{1,0:T(8,128)(2,1)} %cot_ref.1, ...), custom_call_target="tpu_custom_call" | custom-call | tf_op jit(solution)/shard_map/prepare/pallas_call | solution.py:103
  13.9 97.4 %exchange.1 = f32[832,128]{1,0:T(8,128)} custom-call(f32[6664,128]{1,0:T(8,128)} %get-tuple-element.8.grad_ref, s32[64,256]{1,0:T(8,128)} %get-tuple-element.9.src_ref, s32[64,1,256]{2,1,0:T(1,128)} %get-tuple-element.10.key_ref), custom_call_target="tpu_custom_call" | custom-call | tf_op jit(solution)/shard_map/exchange/pallas_call | solution.py:313
  111.3 1.2 %multiply_reduce_fusion = (f32[832]{0:T(1024)S(1)}, f32[832,128]{1,0:T(8,128)S(1)}) fusion(f32[832,128]{1,0:T(8,128)} %exchange.1), kind=kLoop, calls=%fused_computation.1 | loop fusion | flops 318656 | bytes 855296 | tf_op jit(solution)/shard_map/reduce_sum | solution.py:343
  112.6 0.1 div.18
  112.6 0.0 copy-done.1
  112.6 0.6 sqrt_add_fusion
  113.2 0.0 copy-done
  113.2 0.9 divide_subtract_fusion
  (1 shorter events, 0.0 us)
Async XLA Ops:
  0.6 112.0 %copy-start.1 = (f32[26,32]{1,0:T(8,128)S(1)}, f32[26,32]{1,0:T(8,128)}, u32[]{:S(2)}) copy-start(f32[26,32]{1,0:T(8,128)} %param.15) | copy-start | bytes 9988
  0.6 112.6 %copy-start = (f32[26,32,128]{2,1,0:T(8,128)S(1)}, f32[26,32,128]{2,1,0:T(8,128)}, u32[]{:S(2)}) copy-start(f32[26,32,128]{2,1,0:T(8,128)} %param.14) | copy-start | bytes 1277956
